TPU v7x, 32 devices: a whole 2x2x4 slice. The times are simulated.
32 devices in a mesh: ccd: 16 (over z, y, x), row: 2 (over core).
Axes of the slice: x: 2, y: 2, z: 4, core: 2. Of those that a mesh axis runs over, the one named last changes fastest.
Arguments:
- exposure: float32 [16, 48, 2048], P('ccd', 'row'), may hold values from -6 to 6
- row_shift: int32 [16], P('ccd'), may hold values from 0 to 7
- row_fraction: bfloat16 [16, 48], P('ccd', 'row'), may hold values from 0 to 1
- column_shift: int32 [16], P('ccd'), may hold values from 0 to 127
- column_fraction: bfloat16 [16, 2048], P('ccd'), may hold values from 0 to 1
- piece_width: int32 [16, 16], P('ccd'), may hold values from 1 to 128
- route_tile: int32 [16, 16], P('ccd'), may hold values from 0 to 15, as said below
- route_cell: int32 [16, 16], P('ccd'), may hold values from 0 to 31, as said below
- template: float32 [16, 48, 4096], P('ccd', 'row'), may hold values from -6 to 6
- match_kernel: bfloat16 [16, 41, 41], P('ccd'), may hold values from -0.15625 to 0.15625
- detection_kernel: bfloat16 [16, 15, 15], P('ccd'), may hold values from -0.375 to 0.375
Outputs:
- difference: float32 [16, 48, 4096], P('ccd', 'row')
- significance: float32 [16, 48, 4096], P('ccd', 'row')
- noise_level: float32 [], replicated
Inputs may be any that keep to these rules, and one draw needn't show every extreme that they name: Piece p of CCD c lands on tile route_tile[c, p]. Every tile receives at least one piece and at most 32 pieces in all; a quarter of the tiles receive exactly 32. No CCD puts more than 2 pieces on one tile, and some CCDs put exactly 2. `route_cell`: pieces that land on one tile fill different cells.
All inputs are finite; a program needn't handle non-finite values.
Results may differ from a plain program's by a relative error of at most 0.0044.
Values may be sent and summed in bfloat16 or wider, within the bound.
A program may use at most 128 MiB of HBM per device.

v0:
```python
import jax
import jax.numpy as jnp
from jax import lax
from jax.sharding import PartitionSpec as P

PW = 128
PAIR = 2
HALO = 8
KS = 41
DK = 15
stack_depth = 5


def extended_2(x, sides, width):
    for axis, dim in sides:
        size, length = (lax.axis_size(axis), x.shape[dim])
        up = [(i, (i + 1) % size) for i in range(size - 1)]
        down = [(j, i) for i, j in up]
        last = lax.slice_in_dim(x, length - width, length, axis=dim)
        first = lax.slice_in_dim(x, 0, width, axis=dim)
        before = lax.ppermute(last, axis, up)
        after = lax.ppermute(first, axis, down)
        x = jnp.concatenate([before, x, after], axis=dim)
    return x


def passed_along(block, axis, distance):
    devices = range(lax.axis_size(axis))
    route = [(i - distance, i) for i in devices if i - distance in devices]
    return lax.ppermute(block, axis, route)


def warp_columns(padded, column_offset, fraction):
    length = fraction.shape[-1]
    leftward = lax.dynamic_slice_in_dim(padded, column_offset, length, 1).astype(jnp.float32)
    rightward = lax.dynamic_slice_in_dim(padded, column_offset + 1, length, 1).astype(jnp.float32)
    weight = fraction.astype(jnp.float32)[None, :]
    return (1.0 - weight) * leftward + weight * rightward


def band_matrix(kernel):
    extent = kernel.shape[0]
    spread = jnp.arange(2 * PW, dtype=jnp.int32)[:, None] - jnp.arange(PW, dtype=jnp.int32)[None, :]
    picker = (spread[:, :, None] == jnp.arange(extent, dtype=jnp.int32)[None, None, :]).astype(
        jnp.bfloat16
    )
    return jnp.einsum("yd,kjd->ykj", kernel, picker, preferred_element_type=jnp.float32).astype(
        jnp.bfloat16
    )


def banded_filter(source, kernel, height):
    extent = kernel.shape[0]
    margin = extent // 2
    blocks_wide = source.shape[1] // PW
    widened = jnp.pad(source, ((0, 0), (margin, 2 * PW - margin)))
    blocked = widened.reshape(widened.shape[0], blocks_wide + 2, PW)
    windows = jnp.concatenate([blocked[:, :blocks_wide], blocked[:, 1 : blocks_wide + 1]], axis=2)
    banded = band_matrix(kernel)
    running = jnp.zeros((height, blocks_wide, PW), jnp.float32)
    for offset in range(0, extent, stack_depth):
        finish = min(offset + stack_depth, extent)
        stacked = jnp.stack(
            [windows[depth_row : depth_row + height] for depth_row in range(offset, finish)], axis=2
        )
        running = running + jnp.einsum(
            "rcgk,gkj->rcj", stacked, banded[offset:finish], preferred_element_type=jnp.float32
        )
    return running.reshape(height, blocks_wide * PW)


def match_template(template, match_kernel, height):
    rounded = template[0].astype(jnp.bfloat16)
    haloed = extended_2(rounded, (("row", 0),), KS // 2)
    return banded_filter(haloed, match_kernel[0], height)


def detection_pass(difference, detection_kernel, height):
    rounded = difference.astype(jnp.bfloat16)
    haloed = extended_2(rounded, (("row", 0),), DK // 2)
    return banded_filter(haloed, detection_kernel[0], height)


def noise_totals(square_sum, live_count):
    return lax.psum((square_sum, live_count), ("ccd", "row"))


def deliver_pieces(
    exposure,
    row_shift,
    row_fraction,
    column_shift,
    column_fraction,
    piece_width,
    route_tile,
    route_cell,
    cell_count,
):
    exposure_band = exposure[0]
    height = exposure_band.shape[0]
    columns = exposure_band.shape[1]
    pieces = columns // PW
    capacity = lax.axis_size("ccd") * PAIR
    below_rows = passed_along(exposure_band[:HALO], "row", -1)
    extended = jnp.concatenate([exposure_band, below_rows], axis=0)
    weight = row_fraction[0].astype(jnp.float32)[:, None]
    upper_rows = lax.dynamic_slice_in_dim(extended, row_shift[0], height, 0)
    lower_rows = lax.dynamic_slice_in_dim(extended, row_shift[0] + 1, height, 0)
    warped_rows = ((1.0 - weight) * upper_rows + weight * lower_rows).astype(jnp.bfloat16)
    padded = jnp.pad(warped_rows, ((0, 0), (0, PW)))
    piece_tile = route_tile[0]
    piece_cell = route_cell[0]
    widths = piece_width[0]
    order_index = jnp.arange(pieces, dtype=jnp.int32)
    earlier = (piece_tile[:, None] == piece_tile[None, :]) & (
        order_index[None, :] < order_index[:, None]
    )
    piece_rank = jnp.sum(earlier.astype(jnp.int32), axis=1)
    target = piece_tile * PAIR + piece_rank
    chooser = jnp.arange(capacity, dtype=jnp.int32)[:, None] == target[None, :]
    chooser_half = chooser.astype(jnp.bfloat16)
    sent_cell = jnp.sum(jnp.where(chooser, piece_cell[None, :] + 1, 0), axis=1) - 1
    sent_width = jnp.sum(jnp.where(chooser, widths[None, :], 0), axis=1)
    lane_index = jnp.arange(PW, dtype=jnp.int32)
    warped = warp_columns(padded, column_shift[0], column_fraction[0]).astype(jnp.bfloat16)
    keep_mask = (lane_index[None, :] < widths[:, None]).reshape(columns)
    warped = jnp.where(keep_mask[None, :], warped, jnp.zeros((), jnp.bfloat16))
    outgoing = jnp.einsum(
        "sp,rpj->srj",
        chooser_half,
        warped.reshape(height, pieces, PW),
        preferred_element_type=jnp.float32,
    ).astype(jnp.bfloat16)
    incoming, got_cell, got_width = (
        lax.all_to_all(outgoing, "ccd", split_axis=0, concat_axis=0, tiled=True),
        lax.all_to_all(sent_cell, "ccd", split_axis=0, concat_axis=0, tiled=True),
        lax.all_to_all(sent_width, "ccd", split_axis=0, concat_axis=0, tiled=True),
    )
    placer = jnp.arange(cell_count, dtype=jnp.int32)[:, None] == got_cell[None, :]
    science = jnp.einsum(
        "qs,srj->rqj", placer.astype(jnp.bfloat16), incoming, preferred_element_type=jnp.float32
    ).reshape(height, cell_count * PW)
    cell_width = jnp.sum(jnp.where(placer, got_width[None, :], 0), axis=1).astype(jnp.int32)
    live_mask = (lane_index[None, :] < cell_width[:, None]).reshape(cell_count * PW)
    return (science, live_mask, cell_width)


def on_device(
    exposure,
    row_shift,
    row_fraction,
    column_shift,
    column_fraction,
    piece_width,
    route_tile,
    route_cell,
    template,
    match_kernel,
    detection_kernel,
):
    height = exposure.shape[1]
    cell_count = template.shape[2] // PW
    science, live_mask, cell_width = deliver_pieces(
        exposure,
        row_shift,
        row_fraction,
        column_shift,
        column_fraction,
        piece_width,
        route_tile,
        route_cell,
        cell_count,
    )
    matched = match_template(template, match_kernel, height)
    difference = jnp.where(live_mask[None, :], science - matched, jnp.zeros((), jnp.float32))
    square_sum = jnp.sum(difference * difference)
    live_count = (height * jnp.sum(cell_width)).astype(jnp.float32)
    filtered = detection_pass(difference, detection_kernel, height)
    total_square, total_count = noise_totals(square_sum, live_count)
    noise_level = total_square / total_count
    detect_weights = detection_kernel[0].astype(jnp.float32)
    kernel_norm = jnp.sum(detect_weights * detect_weights)
    significance = filtered / jnp.sqrt(1.0 + noise_level * kernel_norm)
    return (difference[None], significance[None], noise_level)


def solution(mesh):
    return jax.shard_map(
        on_device,
        mesh=mesh,
        in_specs=(
            P("ccd", "row", None),
            P("ccd"),
            P("ccd", "row"),
            P("ccd"),
            P("ccd", None),
            P("ccd", None),
            P("ccd", None),
            P("ccd", None),
            P("ccd", "row", None),
            P("ccd", None, None),
            P("ccd", None, None),
        ),
        out_specs=(P("ccd", "row", None), P("ccd", "row", None), P()),
        check_vma=False,
    )
```

profile of v0, /device:TPU:0, one launch (start us, length us, event | category | flops | bytes accessed | tf_op | source)
XLA Modules:
  0.0 126.3 jit_solution(17106949905012191423)
XLA Ops:
  0.6 1.0 convert_element_type.82
  1.7 0.8 slice_bitcast_fusion.10
  2.5 3.1 %collective-permute-start.1 = (bf16[20,4096]{1,0:T(8,128)(2,1)}, bf16[20,4096]{1,0:T(8,128)(2,1)}, u32[]{:S(2)}, u32[]{:S(2)}) collective-permute-start(bf16[20,4096]{1,0:T(8,128)(2,1)} %get-tuple-element.53), channel_id=1, source_target_pairs={{0,1},{2,3},{4,5},{6,7},{8,9},{10,11},{12,13},{14,15},{16,17},{18,... | collective-permute-start | bytes 491528 | tf_op jit(solution)/shard_map/ppermute | solution.py:21
  5.5 1.3 %collective-permute-start.2 = (bf16[20,4096]{1,0:T(8,128)(2,1)}, bf16[20,4096]{1,0:T(8,128)(2,1)}, u32[]{:S(2)}, u32[]{:S(2)}) collective-permute-start(bf16[20,4096]{1,0:T(8,128)(2,1)} %get-tuple-element.54), channel_id=1, source_target_pairs={{1,0},{3,2},{5,4},{7,6},{9,8},{11,10},{13,12},{15,14},{17,16},{19,... | collective-permute-start | bytes 491528 | tf_op jit(solution)/shard_map/ppermute | solution.py:22
  6.8 1.5 %slice_bitcast_fusion.11 = f32[8,2048]{1,0:T(8,128)} fusion(f32[1,24,2048]{2,1,0:T(8,128)} %param.11), kind=kLoop, calls=%fused_computation.369 | loop fusion | bytes 131072 | tf_op jit(solution)/shard_map/slice | solution.py:104
  8.3 1.3 %collective-permute-start = (f32[8,2048]{1,0:T(8,128)}, f32[8,2048]{1,0:T(8,128)}, u32[]{:S(2)}, u32[]{:S(2)}) collective-permute-start(f32[8,2048]{1,0:T(8,128)} %slice_bitcast_fusion.11), channel_id=1, source_target_pairs={{1,0},{3,2},{5,4},{7,6},{9,8},{11,10},{13,12},{15,14},{17,16},{19,... | collective-permute-start | bytes 196616 | tf_op jit(solution)/shard_map/ppermute | solution.py:30
  9.6 0.9 convert_reduce_fusion
  10.5 0.7 fusion.228
  11.7 1.3 select_reduce_fusion.2
  13.0 0.7 sub.70
  13.7 7.7 %all-to-all-start = ((s32[16,2,1]{1,2,0:T(1,128)}), s32[16,2,1]{1,2,0:T(1,128)}, u32[]{:S(2)}, u32[]{:S(2)}) async-start(s32[16,2,1]{1,2,0:T(1,128)} %bitcast.4), calls=%async_computation | async-start | bytes 16384 | tf_op jit(solution)/shard_map/all_to_all | solution.py:136
  21.4 1.0 convert_bitcast_fusion.1
  22.5 1.6 %convert_bitcast_fusion = bf16[41,256,128]{2,0,1:T(8,128)(2,1)S(1)} fusion(s32[256,128]{1,0:T(8,128)S(1)} %iota_subtract_fusion, bf16[1,41,41]{2,1,0:T(8,128)(2,1)S(1)} %copy-done), kind=kOutput, calls=%fused_computation.83 | convolution fusion | flops 112852992 | bytes 2821410 | tf_op jit(solution)/shard_map/yd,kjd->ykj/dot_general | solution.py:47
  24.1 2.2 %fusion.231 = (bf16[5,256,128]{2,0,1:T(8,128)(2,1)S(1)}, bf16[5,256,128,1]{2,0,1,3:T(8,128)(2,1)}, bf16[5,256,128,1]{2,0,1,3:T(8,128)(2,1)}, bf16[5,256,128,1]{2...) fusion(bf16[41,256,128]{2,0,1:T(8,128)(2,1)S(1)} %convert_bitca, ...), kind=kLoop, calls=%fused_computation.398 | loop fusion | bytes 5242880 | tf_op jit(solution)/shard_map/slice | solution.py:67
  26.3 0.7 slice.412
  28.2 0.6 fusion.225
  30.1 0.7 multiply_reduce_fusion.1
  32.7 1.3 %all_to_all.14 = s32[16,2,1]{1,0,2:T(8,128)} reshape(s32[32]{0:T(128)} %get-tuple-element.5) | data formatting | bytes 256 | tf_op jit(solution)/shard_map/all_to_all | solution.py:137
  34.0 1.3 %fusion.232 = (bf16[5,256,128]{2,0,1:T(8,128)(2,1)}, bf16[5,256,128,1]{2,0,1,3:T(8,128)(2,1)}, bf16[5,256,128,1]{2,0,1,3:T(8,128)(2,1)}) fusion(bf16[15,256,128]{2,0,1:T(8,128)(2,1)S(1)} %fusion.4), kind=kLoop, calls=%fused_computation.399 | loop fusion | bytes 1966080 | tf_op jit(solution)/shard_map/slice | solution.py:67
  35.3 6.9 %all-to-all-start.1 = ((s32[16,2,1]{1,2,0:T(1,128)}), s32[16,2,1]{1,2,0:T(1,128)S(1)}, u32[]{:S(2)}, u32[]{:S(2)}) async-start(s32[16,2,1]{1,2,0:T(1,128)} %bitcast.401), calls=%async_computation.1 | async-start | bytes 16384 | tf_op jit(solution)/shard_map/all_to_all | solution.py:137
  42.7 1.4 %reduce.8 = s32[16,2]{1,0:T(8,128)S(1)} reduce(s32[16,2,1]{1,2,0:T(1,128)} %all-to-all-done, s32[]{:T(128)} %broadcast.128), dimensions={2}, to_apply=%all_to_all.13.reduce_sub_computation.3 | reduce | bytes 260 | tf_op jit(solution)/shard_map/all_to_all | solution.py:136
  44.2 5.3 %all-to-all-done.1 = s32[16,2,1]{1,2,0:T(1,128)S(1)} async-done(((s32[16,2,1]{1,2,0:T(1,128)}), s32[16,2,1]{1,2,0:T(1,128)S(1)}, u32[]{:S(2)}, u32[]{:S(2)}) %all-to-all-start.1) | async-done | bytes 160 | tf_op jit(solution)/shard_map/all_to_all | solution.py:137
  49.5 0.7 reduce.9
  51.7 1.1 fusion.210
  52.7 0.8 fusion.215
  53.6 1.0 convolution_convert_fusion
  54.6 0.8 copy.95
  55.4 4.4 %all-to-all-start.2 = ((bf16[32,24,128]{2,1,0:T(8,128)(2,1)}), bf16[32,24,128]{2,1,0:T(8,128)(2,1)}, u32[]{:S(2)}, u32[]{:S(2)}) async-start(bf16[32,24,128]{2,1,0:T(8,128)(2,1)} %copy.95), calls=%async_computation.2 | async-start | bytes 393216 | tf_op jit(solution)/shard_map/all_to_all | solution.py:135
  59.7 1.3 %fusion.23 = bf16[64,4352]{1,0:T(8,128)(2,1)S(1)} fusion(bf16[20,4096]{1,0:T(8,128)(2,1)} %collective-permute-done.2, bf16[24,4096]{1,0:T(8,128)(2,1)S(1)} %convert_bitcast_fusion.1, bf16[20,4096]{1,0:T(8,128)(2,1)} %collective-permute-done.1), kind=kLoop, calls=%fused_computation.153 | loop fusion | flops 3342336 | bytes 1081344 | tf_op jit(solution)/shard_map/concatenate | solution.py:23
  63.8 0.7 copy-done.4
  64.5 0.7 convolution_bitcast_fusion.3
  65.1 0.7 convolution_bitcast_fusion.4
  66.2 0.7 convolution_bitcast_fusion.5
  66.9 0.7 convolution_bitcast_fusion.6
  67.6 0.7 convolution_bitcast_fusion.7
  68.3 0.7 convolution_bitcast_fusion.8
  69.0 0.7 convolution_bitcast_fusion.9
  69.6 0.8 fusion.12
  70.8 1.8 %multiply_reduce_fusion = (f32[]{:T(128)}, f32[24,32,128]{2,1,0:T(8,128)S(1)}) fusion(pred[32,128]{1,0:T(8,128)(4,1)S(1)} %get-tuple-element.55, f32[24,32,128]{2,1,0:T(8,128)S(1)} %convolution_add_fusion, s32[32]{0:T(128)S(1)} %eq.80, bf16[32,24,128]{2,1,0:T(8,128)(2,1)} %all-to-all-done.2), kind=kOutput, calls=%fused_computation.333 | convolution fusion | flops 6685695 | bytes 987268 | tf_op jit(solution)/shard_map/qs,srj->rqj/dot_general | solution.py:140
  72.9 2.3 %collective-permute-start.3 = (bf16[7,4096]{1,0:T(8,128)(2,1)S(1)}, bf16[7,4096]{1,0:T(8,128)(2,1)S(1)}, u32[]{:S(2)}, u32[]{:S(2)}) collective-permute-start(bf16[7,4096]{1,0:T(8,128)(2,1)S(1)} %get-tuple-element.51), channel_id=1, source_target_pairs={{0,1},{2,3},{4,5},{6,7},{8,9},{10,11},{12,13},{14,15},{16,17},{18,... | collective-permute-start | bytes 172040 | tf_op jit(solution)/shard_map/ppermute | solution.py:21
  75.3 1.3 %collective-permute-start.4 = (bf16[7,4096]{1,0:T(8,128)(2,1)S(1)}, bf16[7,4096]{1,0:T(8,128)(2,1)S(1)}, u32[]{:S(2)}, u32[]{:S(2)}) collective-permute-start(bf16[7,4096]{1,0:T(8,128)(2,1)S(1)} %get-tuple-element.52), channel_id=1, source_target_pairs={{1,0},{3,2},{5,4},{7,6},{9,8},{11,10},{13,12},{15,14},{17,16},{19,... | collective-permute-start | bytes 172040 | tf_op jit(solution)/shard_map/ppermute | solution.py:22
  76.6 0.8 broadcast_select_fusion
  77.4 40.2 %all-reduce.3 = (f32[]{:T(128)}, f32[]{:T(128)}) all-reduce(f32[]{:T(128)} %get-tuple-element.57, f32[]{:T(128)S(6)} %convert_element_type.89), channel_id=1, replica_groups=mesh['ccd'=16,'row'=2] {'ccd','row'}, use_global_device_ids=true, to_apply=%region_5.6 | all-reduce | flops 2 | bytes 16 | tf_op jit(solution)/shard_map/psum | solution.py:85
  121.1 0.8 copy-done.6
  121.9 0.7 convolution_bitcast_fusion
  122.6 0.7 convolution_bitcast_fusion.1
  123.7 0.7 fusion.15
  124.4 0.8 div.22
  (91 shorter events, 10.5 us)
Async XLA Ops:
  0.6 21.8 %copy-start = (bf16[1,41,41]{2,1,0:T(8,128)(2,1)S(1)}, bf16[1,41,41]{2,1,0:T(8,128)(2,1)}, u32[]{:S(2)}) copy-start(bf16[1,41,41]{2,1,0:T(8,128)(2,1)} %param.20) | copy-start | bytes 10090
  2.5 57.3 %collective-permute-start.1 = (bf16[20,4096]{1,0:T(8,128)(2,1)}, bf16[20,4096]{1,0:T(8,128)(2,1)}, u32[]{:S(2)}, u32[]{:S(2)}) collective-permute-start(bf16[20,4096]{1,0:T(8,128)(2,1)} %get-tuple-element.53), channel_id=1, source_target_pairs={{0,1},{2,3},{4,5},{6,7},{8,9},{10,11},{12,13},{14,15},{16,17},{18,... | collective-permute-start | bytes 491528 | tf_op jit(solution)/shard_map/ppermute | solution.py:21
  5.5 54.2 %collective-permute-start.2 = (bf16[20,4096]{1,0:T(8,128)(2,1)}, bf16[20,4096]{1,0:T(8,128)(2,1)}, u32[]{:S(2)}, u32[]{:S(2)}) collective-permute-start(bf16[20,4096]{1,0:T(8,128)(2,1)} %get-tuple-element.54), channel_id=1, source_target_pairs={{1,0},{3,2},{5,4},{7,6},{9,8},{11,10},{13,12},{15,14},{17,16},{19,... | collective-permute-start | bytes 491528 | tf_op jit(solution)/shard_map/ppermute | solution.py:22
  8.3 43.4 %collective-permute-start = (f32[8,2048]{1,0:T(8,128)}, f32[8,2048]{1,0:T(8,128)}, u32[]{:S(2)}, u32[]{:S(2)}) collective-permute-start(f32[8,2048]{1,0:T(8,128)} %slice_bitcast_fusion.11), channel_id=1, source_target_pairs={{1,0},{3,2},{5,4},{7,6},{9,8},{11,10},{13,12},{15,14},{17,16},{19,... | collective-permute-start | bytes 196616 | tf_op jit(solution)/shard_map/ppermute | solution.py:30
  11.2 0.6 copy-start.12
  13.7 21.7 %all-to-all-start = ((s32[16,2,1]{1,2,0:T(1,128)}), s32[16,2,1]{1,2,0:T(1,128)}, u32[]{:S(2)}, u32[]{:S(2)}) async-start(s32[16,2,1]{1,2,0:T(1,128)} %bitcast.4), calls=%async_computation | async-start | bytes 16384 | tf_op jit(solution)/shard_map/all_to_all | solution.py:136
  24.0 3.0 %copy-start.14 = (bf16[1,24]{1,0:T(2,128)(2,1)S(1)}, bf16[1,24]{1,0:T(2,128)(2,1)}, u32[]{:S(2)}) copy-start(bf16[1,24]{1,0:T(2,128)(2,1)} %param.13) | copy-start | bytes 148
  24.1 4.2 %copy-start.13 = (s32[1,16]{1,0:T(1,128)S(1)}, s32[1,16]{1,0:T(1,128)}, u32[]{:S(2)}) copy-start(s32[1,16]{1,0:T(1,128)} %param.16) | copy-start | bytes 196
  24.1 4.8 %copy-start.10 = (bf16[1,2048]{1,0:T(2,128)(2,1)S(1)}, bf16[1,2048]{1,0:T(2,128)(2,1)}, u32[]{:S(2)}) copy-start(bf16[1,2048]{1,0:T(2,128)(2,1)} %param.15) | copy-start | bytes 12292
  24.1 6.0 %copy-start.11 = (bf16[1,15,15]{2,1,0:T(8,128)(2,1)S(1)}, bf16[1,15,15]{2,1,0:T(8,128)(2,1)}, u32[]{:S(2)}) copy-start(bf16[1,15,15]{2,1,0:T(8,128)(2,1)} %param.21) | copy-start | bytes 1354
  30.7 20.9 %copy-start.8 = (f32[1,24,2048]{2,1,0:T(8,128)S(1)}, f32[1,24,2048]{2,1,0:T(8,128)}, u32[]{:S(2)}) copy-start(f32[1,24,2048]{2,1,0:T(8,128)} %param.11) | copy-start | bytes 589828
  35.3 14.2 %all-to-all-start.1 = ((s32[16,2,1]{1,2,0:T(1,128)}), s32[16,2,1]{1,2,0:T(1,128)S(1)}, u32[]{:S(2)}, u32[]{:S(2)}) async-start(s32[16,2,1]{1,2,0:T(1,128)} %bitcast.401), calls=%async_computation.1 | async-start | bytes 16384 | tf_op jit(solution)/shard_map/all_to_all | solution.py:137
  55.4 15.5 %all-to-all-start.2 = ((bf16[32,24,128]{2,1,0:T(8,128)(2,1)}), bf16[32,24,128]{2,1,0:T(8,128)(2,1)}, u32[]{:S(2)}, u32[]{:S(2)}) async-start(bf16[32,24,128]{2,1,0:T(8,128)(2,1)} %copy.95), calls=%async_computation.2 | async-start | bytes 393216 | tf_op jit(solution)/shard_map/all_to_all | solution.py:135
  63.4 1.0 copy-start.4
  63.6 1.5 %copy-start.3 = (bf16[5,256,128,1]{2,0,1,3:T(8,128)(2,1)S(1)}, bf16[5,256,128,1]{2,0,1,3:T(8,128)(2,1)}, u32[]{:S(2)}) copy-start(bf16[5,256,128,1]{2,0,1,3:T(8,128)(2,1)} %get-tuple-element.11) | copy-start | bytes 983044
  65.1 1.0 copy-start.2
  65.8 1.1 copy-start.1
  69.6 0.9 copy-start.9
  72.9 46.7 %collective-permute-start.3 = (bf16[7,4096]{1,0:T(8,128)(2,1)S(1)}, bf16[7,4096]{1,0:T(8,128)(2,1)S(1)}, u32[]{:S(2)}, u32[]{:S(2)}) collective-permute-start(bf16[7,4096]{1,0:T(8,128)(2,1)S(1)} %get-tuple-element.51), channel_id=1, source_target_pairs={{0,1},{2,3},{4,5},{6,7},{8,9},{10,11},{12,13},{14,15},{16,17},{18,... | collective-permute-start | bytes 172040 | tf_op jit(solution)/shard_map/ppermute | solution.py:21
  75.3 44.3 %collective-permute-start.4 = (bf16[7,4096]{1,0:T(8,128)(2,1)S(1)}, bf16[7,4096]{1,0:T(8,128)(2,1)S(1)}, u32[]{:S(2)}, u32[]{:S(2)}) collective-permute-start(bf16[7,4096]{1,0:T(8,128)(2,1)S(1)} %get-tuple-element.52), channel_id=1, source_target_pairs={{1,0},{3,2},{5,4},{7,6},{9,8},{11,10},{13,12},{15,14},{17,16},{19,... | collective-permute-start | bytes 172040 | tf_op jit(solution)/shard_map/ppermute | solution.py:22
  120.9 1.1 copy-start.6
  121.1 1.6 %copy-start.5 = (bf16[5,256,128,1]{2,0,1,3:T(8,128)(2,1)S(1)}, bf16[5,256,128,1]{2,0,1,3:T(8,128)(2,1)}, u32[]{:S(2)}) copy-start(bf16[5,256,128,1]{2,0,1,3:T(8,128)(2,1)} %get-tuple-element.19) | copy-start | bytes 983044
  122.6 1.0 copy-start.7
where the time goes:
time: 127 us; the launch traced here: 126 us
  blocking collectives  40.2 us (32%)
  starting transfers between devices  28.2 us (22%)
  other arithmetic  18.6 us (15%)
  local copies, waits for them, and re-layouts  14.7 us (12%)
  matrix products  12.8 us (10%)
  between operations  6.44 us (5%)
  waiting for transfers between devices  5.34 us (4%)
    psum x1, blocking collectives, noise_totals(): return lax.psum((square_sum, live_count), ('ccd', 'row'))  40.2 us
    dot_general x12, matrix products, banded_filter(): jnp.einsum('rcgk,gkj->rcj', stacked, banded[offset:finish], preferred_ele...  7.79 us
    all_to_all x1, starting transfers between devices, deliver_pieces(): lax.all_to_all(sent_cell, 'ccd', split_axis=0, concat_axis=0, tiled=True)  7.73 us
    all_to_all x1, starting transfers between devices, deliver_pieces(): lax.all_to_all(sent_width, 'ccd', split_axis=0, concat_axis=0, tiled=True)  6.86 us
    ppermute x2, starting transfers between devices, extended_2(): before = lax.ppermute(last, axis, up)  5.4 us
    all_to_all x1, waiting for transfers between devices, deliver_pieces(): lax.all_to_all(sent_width, 'ccd', split_axis=0, concat_axis=0, tiled=True)  5.33 us
    all_to_all x1, starting transfers between devices, deliver_pieces(): lax.all_to_all(outgoing, 'ccd', split_axis=0, concat_axis=0, tiled=True)  4.35 us
    slice x3, local copies, waits for them, and re-layouts, banded_filter(): banded[offset:finish]  4.24 us
  transfers between devices with their start and end apart: 8, of which 1 were waited for; matrix products, arithmetic and copies ran while one was open for 27% of the time, Pallas kernels for 0%

commit v1 on v0

--- a/solution.py
+++ b/solution.py
@@ -82,7 +82,7 @@
 
 
 def noise_totals(square_sum, live_count):
-    return lax.psum((square_sum, live_count), ("ccd", "row"))
+    return lax.psum(lax.psum((square_sum, live_count), "ccd"), "row")
 
 
 def deliver_pieces(

time: 127 us -> 132 us (1.039)
  blocking collectives: 40.2 us -> 45.2 us
    psum x1 -> x2, blocking collectives: 40.2 us -> 45.2 us  [noise_totals(): return lax.psum(lax.psum((square_sum, live_count), 'ccd'), 'row')]
  transfers between devices with their start and end apart: 8 -> 8, of which waited for: 1 -> 1; matrix products, arithmetic and copies ran while one was open for 27% -> 26% of each run, Pallas kernels for 0% -> 0%
where the time goes in v1:
time: 132 us; the launch traced here: 131 us
  blocking collectives  45.2 us (34%)
  starting transfers between devices  28.2 us (21%)
  other arithmetic  18.5 us (14%)
  local copies, waits for them, and re-layouts  14.7 us (11%)
  matrix products  12.7 us (10%)
  between operations  6.43 us (5%)
  waiting for transfers between devices  5.33 us (4%)
    psum x2, blocking collectives, noise_totals(): return lax.psum(lax.psum((square_sum, live_count), 'ccd'), 'row')  45.2 us
    dot_general x12, matrix products, banded_filter(): jnp.einsum('rcgk,gkj->rcj', stacked, banded[offset:finish], preferred_ele...  7.78 us
    all_to_all x1, starting transfers between devices, deliver_pieces(): lax.all_to_all(sent_cell, 'ccd', split_axis=0, concat_axis=0, tiled=True)  7.73 us
    all_to_all x1, starting transfers between devices, deliver_pieces(): lax.all_to_all(sent_width, 'ccd', split_axis=0, concat_axis=0, tiled=True)  6.85 us
    ppermute x2, starting transfers between devices, extended_2(): before = lax.ppermute(last, axis, up)  5.39 us
    all_to_all x1, waiting for transfers between devices, deliver_pieces(): lax.all_to_all(sent_width, 'ccd', split_axis=0, concat_axis=0, tiled=True)  5.32 us
    all_to_all x1, starting transfers between devices, deliver_pieces(): lax.all_to_all(outgoing, 'ccd', split_axis=0, concat_axis=0, tiled=True)  4.35 us
    slice x3, local copies, waits for them, and re-layouts, banded_filter(): banded[offset:finish]  4.23 us
  transfers between devices with their start and end apart: 8, of which 1 were waited for; matrix products, arithmetic and copies ran while one was open for 26% of the time, Pallas kernels for 0%

profile of v1, /device:TPU:0, one launch (start us, length us, event | category | flops | bytes accessed | tf_op | source)
XLA Modules:
  0.0 131.0 jit_solution(15532439059084303233)
XLA Ops:
  0.6 1.0 convert_element_type.82
  1.7 0.8 slice_bitcast_fusion.10
  2.5 3.1 %collective-permute-start.1 = (bf16[20,4096]{1,0:T(8,128)(2,1)}, bf16[20,4096]{1,0:T(8,128)(2,1)}, u32[]{:S(2)}, u32[]{:S(2)}) collective-permute-start(bf16[20,4096]{1,0:T(8,128)(2,1)} %get-tuple-element.55), channel_id=1, source_target_pairs={{0,1},{2,3},{4,5},{6,7},{8,9},{10,11},{12,13},{14,15},{16,17},{18,... | collective-permute-start | bytes 491528 | tf_op jit(solution)/shard_map/ppermute | solution.py:21
  5.5 1.3 collective-permute-start.2
  6.8 1.5 %slice_bitcast_fusion.11 = f32[8,2048]{1,0:T(8,128)} fusion(f32[1,24,2048]{2,1,0:T(8,128)} %param.11), kind=kLoop, calls=%fused_computation.369 | loop fusion | bytes 131072 | tf_op jit(solution)/shard_map/slice | solution.py:104
  8.3 1.3 collective-permute-start
  9.6 0.9 convert_reduce_fusion
  10.5 0.7 fusion.228
  11.7 1.3 select_reduce_fusion.2
  12.9 0.7 sub.70
  13.6 7.7 %all-to-all-start = ((s32[16,2,1]{1,2,0:T(1,128)}), s32[16,2,1]{1,2,0:T(1,128)}, u32[]{:S(2)}, u32[]{:S(2)}) async-start(s32[16,2,1]{1,2,0:T(1,128)} %bitcast.4), calls=%async_computation | async-start | bytes 16384 | tf_op jit(solution)/shard_map/all_to_all | solution.py:136
  21.4 1.0 convert_bitcast_fusion.1
  22.4 1.6 %convert_bitcast_fusion = bf16[41,256,128]{2,0,1:T(8,128)(2,1)S(1)} fusion(s32[256,128]{1,0:T(8,128)S(1)} %iota_subtract_fusion, bf16[1,41,41]{2,1,0:T(8,128)(2,1)S(1)} %copy-done), kind=kOutput, calls=%fused_computation.83 | convolution fusion | flops 112852992 | bytes 2821410 | tf_op jit(solution)/shard_map/yd,kjd->ykj/dot_general | solution.py:47
  24.0 2.2 %fusion.231 = (bf16[5,256,128]{2,0,1:T(8,128)(2,1)S(1)}, bf16[5,256,128,1]{2,0,1,3:T(8,128)(2,1)}, bf16[5,256,128,1]{2,0,1,3:T(8,128)(2,1)}, bf16[5,256,128,1]{2...) fusion(bf16[41,256,128]{2,0,1:T(8,128)(2,1)S(1)} %convert_bitca, ...), kind=kLoop, calls=%fused_computation.398 | loop fusion | bytes 5242880 | tf_op jit(solution)/shard_map/slice | solution.py:67
  26.3 0.7 slice.412
  28.1 0.6 fusion.225
  32.5 1.3 %all_to_all.14 = s32[16,2,1]{1,0,2:T(8,128)} reshape(s32[32]{0:T(128)} %get-tuple-element.5) | data formatting | bytes 256 | tf_op jit(solution)/shard_map/all_to_all | solution.py:137
  33.9 1.3 fusion.232
  35.2 6.9 %all-to-all-start.1 = ((s32[16,2,1]{1,2,0:T(1,128)}), s32[16,2,1]{1,2,0:T(1,128)S(1)}, u32[]{:S(2)}, u32[]{:S(2)}) async-start(s32[16,2,1]{1,2,0:T(1,128)} %bitcast.401), calls=%async_computation.1 | async-start | bytes 16384 | tf_op jit(solution)/shard_map/all_to_all | solution.py:137
  42.5 1.4 %reduce.8 = s32[16,2]{1,0:T(8,128)S(1)} reduce(s32[16,2,1]{1,2,0:T(1,128)} %all-to-all-done, s32[]{:T(128)} %broadcast.128), dimensions={2}, to_apply=%all_to_all.13.reduce_sub_computation.3 | reduce | bytes 260 | tf_op jit(solution)/shard_map/all_to_all | solution.py:136
  44.0 5.3 %all-to-all-done.1 = s32[16,2,1]{1,2,0:T(1,128)S(1)} async-done(((s32[16,2,1]{1,2,0:T(1,128)}), s32[16,2,1]{1,2,0:T(1,128)S(1)}, u32[]{:S(2)}, u32[]{:S(2)}) %all-to-all-start.1) | async-done | bytes 160 | tf_op jit(solution)/shard_map/all_to_all | solution.py:137
  49.3 0.7 reduce.9
  51.5 1.1 fusion.210
  52.5 0.8 fusion.215
  53.4 0.9 convolution_convert_fusion
  54.3 0.8 copy.95
  55.1 4.4 %all-to-all-start.2 = ((bf16[32,24,128]{2,1,0:T(8,128)(2,1)}), bf16[32,24,128]{2,1,0:T(8,128)(2,1)}, u32[]{:S(2)}, u32[]{:S(2)}) async-start(bf16[32,24,128]{2,1,0:T(8,128)(2,1)} %copy.95), calls=%async_computation.2 | async-start | bytes 393216 | tf_op jit(solution)/shard_map/all_to_all | solution.py:135
  59.5 1.3 %fusion.23 = bf16[64,4352]{1,0:T(8,128)(2,1)S(1)} fusion(bf16[20,4096]{1,0:T(8,128)(2,1)} %collective-permute-done.2, bf16[24,4096]{1,0:T(8,128)(2,1)S(1)} %convert_bitcast_fusion.1, bf16[20,4096]{1,0:T(8,128)(2,1)} %collective-permute-done.1), kind=kLoop, calls=%fused_computation.153 | loop fusion | flops 3342336 | bytes 1081344 | tf_op jit(solution)/shard_map/concatenate | solution.py:23
  63.5 0.7 copy-done.4
  64.2 0.7 convolution_bitcast_fusion.3
  64.9 0.7 convolution_bitcast_fusion.4
  65.9 0.7 convolution_bitcast_fusion.5
  66.7 0.7 convolution_bitcast_fusion.6
  67.3 0.7 convolution_bitcast_fusion.7
  68.0 0.7 convolution_bitcast_fusion.8
  68.7 0.7 convolution_bitcast_fusion.9
  69.4 0.8 fusion.12
  70.6 1.8 %multiply_reduce_fusion = (f32[]{:T(128)}, f32[24,32,128]{2,1,0:T(8,128)S(1)}) fusion(pred[32,128]{1,0:T(8,128)(4,1)S(1)} %get-tuple-element.57, f32[24,32,128]{2,1,0:T(8,128)S(1)} %convolution_add_fusion, s32[32]{0:T(128)S(1)} %eq.80, bf16[32,24,128]{2,1,0:T(8,128)(2,1)} %all-to-all-done.2), kind=kOutput, calls=%fused_computation.333 | convolution fusion | flops 6685695 | bytes 987268 | tf_op jit(solution)/shard_map/qs,srj->rqj/dot_general | solution.py:140
  72.7 2.3 %collective-permute-start.3 = (bf16[7,4096]{1,0:T(8,128)(2,1)S(1)}, bf16[7,4096]{1,0:T(8,128)(2,1)S(1)}, u32[]{:S(2)}, u32[]{:S(2)}) collective-permute-start(bf16[7,4096]{1,0:T(8,128)(2,1)S(1)} %get-tuple-element.53), channel_id=1, source_target_pairs={{0,1},{2,3},{4,5},{6,7},{8,9},{10,11},{12,13},{14,15},{16,17},{18,... | collective-permute-start | bytes 172040 | tf_op jit(solution)/shard_map/ppermute | solution.py:21
  75.0 1.3 collective-permute-start.4
  76.3 0.8 broadcast_select_fusion
  77.1 42.2 %all-reduce.3 = (f32[]{:T(128)}, f32[]{:T(128)}) all-reduce(f32[]{:T(128)} %get-tuple-element.59, f32[]{:T(128)S(6)} %convert_element_type.89), channel_id=1, replica_groups=mesh['ccd'=16,'row'=2] {'ccd'}, use_global_device_ids=true, to_apply=%region_5.6 | all-reduce | flops 2 | bytes 16 | tf_op jit(solution)/shard_map/psum | solution.py:85
  119.3 3.1 %all-reduce.4 = (f32[]{:T(128)}, f32[]{:T(128)}) all-reduce(f32[]{:T(128)} %get-tuple-element.7, f32[]{:T(128)} %get-tuple-element.8), channel_id=1, replica_groups=mesh['ccd'=16,'row'=2] {'row'}, use_global_device_ids=true, to_apply=%region_6.7 | all-reduce | flops 2 | bytes 16 | tf_op jit(solution)/shard_map/psum | solution.py:85
  125.9 0.8 copy-done.6
  126.7 0.7 convolution_bitcast_fusion
  127.4 0.7 convolution_bitcast_fusion.1
  128.4 0.7 fusion.15
  129.1 0.8 div.22
  (92 shorter events, 11.0 us)
Async XLA Ops:
  0.6 21.8 %copy-start = (bf16[1,41,41]{2,1,0:T(8,128)(2,1)S(1)}, bf16[1,41,41]{2,1,0:T(8,128)(2,1)}, u32[]{:S(2)}) copy-start(bf16[1,41,41]{2,1,0:T(8,128)(2,1)} %param.20) | copy-start | bytes 10090
  2.5 57.0 %collective-permute-start.1 = (bf16[20,4096]{1,0:T(8,128)(2,1)}, bf16[20,4096]{1,0:T(8,128)(2,1)}, u32[]{:S(2)}, u32[]{:S(2)}) collective-permute-start(bf16[20,4096]{1,0:T(8,128)(2,1)} %get-tuple-element.55), channel_id=1, source_target_pairs={{0,1},{2,3},{4,5},{6,7},{8,9},{10,11},{12,13},{14,15},{16,17},{18,... | collective-permute-start | bytes 491528 | tf_op jit(solution)/shard_map/ppermute | solution.py:21
  5.5 54.0 %collective-permute-start.2 = (bf16[20,4096]{1,0:T(8,128)(2,1)}, bf16[20,4096]{1,0:T(8,128)(2,1)}, u32[]{:S(2)}, u32[]{:S(2)}) collective-permute-start(bf16[20,4096]{1,0:T(8,128)(2,1)} %get-tuple-element.56), channel_id=1, source_target_pairs={{1,0},{3,2},{5,4},{7,6},{9,8},{11,10},{13,12},{15,14},{17,16},{19,... | collective-permute-start | bytes 491528 | tf_op jit(solution)/shard_map/ppermute | solution.py:22
  8.3 43.2 %collective-permute-start = (f32[8,2048]{1,0:T(8,128)}, f32[8,2048]{1,0:T(8,128)}, u32[]{:S(2)}, u32[]{:S(2)}) collective-permute-start(f32[8,2048]{1,0:T(8,128)} %slice_bitcast_fusion.11), channel_id=1, source_target_pairs={{1,0},{3,2},{5,4},{7,6},{9,8},{11,10},{13,12},{15,14},{17,16},{19,... | collective-permute-start | bytes 196616 | tf_op jit(solution)/shard_map/ppermute | solution.py:30
  11.2 0.5 copy-start.12
  13.6 21.5 %all-to-all-start = ((s32[16,2,1]{1,2,0:T(1,128)}), s32[16,2,1]{1,2,0:T(1,128)}, u32[]{:S(2)}, u32[]{:S(2)}) async-start(s32[16,2,1]{1,2,0:T(1,128)} %bitcast.4), calls=%async_computation | async-start | bytes 16384 | tf_op jit(solution)/shard_map/all_to_all | solution.py:136
  24.0 3.0 %copy-start.14 = (bf16[1,24]{1,0:T(2,128)(2,1)S(1)}, bf16[1,24]{1,0:T(2,128)(2,1)}, u32[]{:S(2)}) copy-start(bf16[1,24]{1,0:T(2,128)(2,1)} %param.13) | copy-start | bytes 148
  24.0 4.1 %copy-start.13 = (s32[1,16]{1,0:T(1,128)S(1)}, s32[1,16]{1,0:T(1,128)}, u32[]{:S(2)}) copy-start(s32[1,16]{1,0:T(1,128)} %param.16) | copy-start | bytes 196
  24.0 4.7 %copy-start.10 = (bf16[1,2048]{1,0:T(2,128)(2,1)S(1)}, bf16[1,2048]{1,0:T(2,128)(2,1)}, u32[]{:S(2)}) copy-start(bf16[1,2048]{1,0:T(2,128)(2,1)} %param.15) | copy-start | bytes 12292
  24.0 5.9 %copy-start.11 = (bf16[1,15,15]{2,1,0:T(8,128)(2,1)S(1)}, bf16[1,15,15]{2,1,0:T(8,128)(2,1)}, u32[]{:S(2)}) copy-start(bf16[1,15,15]{2,1,0:T(8,128)(2,1)} %param.21) | copy-start | bytes 1354
  30.6 20.9 %copy-start.8 = (f32[1,24,2048]{2,1,0:T(8,128)S(1)}, f32[1,24,2048]{2,1,0:T(8,128)}, u32[]{:S(2)}) copy-start(f32[1,24,2048]{2,1,0:T(8,128)} %param.11) | copy-start | bytes 589828
  35.2 14.2 %all-to-all-start.1 = ((s32[16,2,1]{1,2,0:T(1,128)}), s32[16,2,1]{1,2,0:T(1,128)S(1)}, u32[]{:S(2)}, u32[]{:S(2)}) async-start(s32[16,2,1]{1,2,0:T(1,128)} %bitcast.401), calls=%async_computation.1 | async-start | bytes 16384 | tf_op jit(solution)/shard_map/all_to_all | solution.py:137
  55.1 15.5 %all-to-all-start.2 = ((bf16[32,24,128]{2,1,0:T(8,128)(2,1)}), bf16[32,24,128]{2,1,0:T(8,128)(2,1)}, u32[]{:S(2)}, u32[]{:S(2)}) async-start(bf16[32,24,128]{2,1,0:T(8,128)(2,1)} %copy.95), calls=%async_computation.2 | async-start | bytes 393216 | tf_op jit(solution)/shard_map/all_to_all | solution.py:135
  63.2 1.0 copy-start.4
  63.4 1.5 %copy-start.3 = (bf16[5,256,128,1]{2,0,1,3:T(8,128)(2,1)S(1)}, bf16[5,256,128,1]{2,0,1,3:T(8,128)(2,1)}, u32[]{:S(2)}) copy-start(bf16[5,256,128,1]{2,0,1,3:T(8,128)(2,1)} %get-tuple-element.13) | copy-start | bytes 983044
  64.9 1.0 copy-start.2
  65.6 1.1 copy-start.1
  69.4 0.9 copy-start.9
  72.7 51.7 %collective-permute-start.3 = (bf16[7,4096]{1,0:T(8,128)(2,1)S(1)}, bf16[7,4096]{1,0:T(8,128)(2,1)S(1)}, u32[]{:S(2)}, u32[]{:S(2)}) collective-permute-start(bf16[7,4096]{1,0:T(8,128)(2,1)S(1)} %get-tuple-element.53), channel_id=1, source_target_pairs={{0,1},{2,3},{4,5},{6,7},{8,9},{10,11},{12,13},{14,15},{16,17},{18,... | collective-permute-start | bytes 172040 | tf_op jit(solution)/shard_map/ppermute | solution.py:21
  75.0 49.3 %collective-permute-start.4 = (bf16[7,4096]{1,0:T(8,128)(2,1)S(1)}, bf16[7,4096]{1,0:T(8,128)(2,1)S(1)}, u32[]{:S(2)}, u32[]{:S(2)}) collective-permute-start(bf16[7,4096]{1,0:T(8,128)(2,1)S(1)} %get-tuple-element.54), channel_id=1, source_target_pairs={{1,0},{3,2},{5,4},{7,6},{9,8},{11,10},{13,12},{15,14},{17,16},{19,... | collective-permute-start | bytes 172040 | tf_op jit(solution)/shard_map/ppermute | solution.py:22
  125.6 1.1 copy-start.6
  125.8 1.6 %copy-start.5 = (bf16[5,256,128,1]{2,0,1,3:T(8,128)(2,1)S(1)}, bf16[5,256,128,1]{2,0,1,3:T(8,128)(2,1)}, u32[]{:S(2)}) copy-start(bf16[5,256,128,1]{2,0,1,3:T(8,128)(2,1)} %get-tuple-element.21) | copy-start | bytes 983044
  127.4 1.0 copy-start.7
